TPU v7x, 32 devices: a whole 2x2x4 slice. The times are simulated.
32 devices in a mesh: grp: 8 (over z, x), dom: 4 (over y, core).
Axes of the slice: x: 2, y: 2, z: 4, core: 2. Of those that a mesh axis runs over, the one named last changes fastest.
Arguments:
- positions: float32 [3, 4096, 512], P(None, ('grp', 'dom')), may hold values from 0 to 1
- velocities: float32 [3, 4096, 512], P(None, ('grp', 'dom')), may hold values from -6 to 6
- masses: float32 [4096, 512], P(('grp', 'dom')), may hold values from 0.5 to 2
- block_halo: int32 [4096], P(('grp', 'dom')), may hold values from 0 to 4095, as said below
- block_shift: int32 [3, 4096], P(None, ('grp', 'dom')), may hold values from -1 to 1
- block_live: int32 [4096], P(('grp', 'dom')), may hold values from 64 to 512
- block_count: int32 [32], P(('grp', 'dom')), may hold values from 32 to 128
- home_slot: int32 [4096], replicated, may hold values from 0 to 4095, as said below
Outputs:
- halo_table: float32 [11, 4096], P(None, ('grp', 'dom'))
- kinetic: float32 [4096, 512], P(('grp', 'dom'))
- radial: float32 [4096, 512], P(('grp', 'dom'))
Inputs may be any that keep to these rules, and one draw needn't show every extreme that they name: A permutation: the halo h is owned by the device of index home_slot[h] // 128 (grp+dom order), in its column home_slot[h] % 128. `block_halo`: the owner of a block's halo lies in the block's own index of grp or in the next one (index + 1, wrapping around); both occur.
All inputs are finite; a program needn't handle non-finite values.
Results may differ from a plain program's by a relative error of at most 0.0003.
Values sent between devices are 32-bit elements; how exact they have to be, the bound alone decides.
No kernel may reach another device: no remote copies, remote signals or barrier semaphores. Data moves between devices by JAX's collectives and lax.ppermute only.
A program may use at most 64 MiB of HBM per device.

v0:
```python
import jax
import jax.numpy as jnp
from jax import lax
from jax.sharding import PartitionSpec as P

BOX = 1.0
EPSILON = 1e-06


def from_behind(shard, axis, by):
    devices = lax.axis_size(axis)
    return lax.ppermute(shard, axis, [(i, (i + by) % devices) for i in range(devices)])


def crossed(first, second):
    return jnp.stack(
        [
            first[1] * second[2] - first[2] * second[1],
            first[2] * second[0] - first[0] * second[2],
            first[0] * second[1] - first[1] * second[0],
        ]
    )


def block_moments(positions, velocities, masses, block_shift, block_live, valid):
    lanes = jnp.arange(masses.shape[1], dtype=jnp.int32)
    live_mask = ((lanes[None, :] < block_live[:, None]) & valid[:, None]).astype(masses.dtype)
    weights = masses * live_mask
    unwrapped = positions + BOX * block_shift.astype(positions.dtype)[:, :, None]
    speed_sq = jnp.sum(velocities * velocities, axis=0)
    angular = crossed(unwrapped, velocities)
    rows = [
        jnp.sum(weights, axis=1)[None],
        jnp.sum(weights * unwrapped, axis=2),
        jnp.sum(weights * velocities, axis=2),
        jnp.sum(weights * speed_sq, axis=1)[None],
        jnp.sum(weights * angular, axis=2),
    ]
    return (jnp.concatenate(rows, axis=0), live_mask, unwrapped)


def halo_properties(sums, total, halos):
    heavy = jnp.maximum(sums[0], 1.0)
    centre = sums[1:4] / heavy
    drift = sums[4:7] / heavy
    spread = sums[7] / heavy - jnp.sum(drift * drift, axis=0)
    spin = sums[8:11] / heavy - crossed(centre, drift)
    share = sums[0] * halos / total
    return jnp.concatenate([share[None], centre, drift, spread[None], spin], axis=0)


def particle_outputs(unwrapped, velocities, live_mask, stats):
    centre = stats[0:3][:, :, None]
    drift = stats[3:6][:, :, None]
    spread = stats[6][:, None]
    offset = velocities - drift
    kinetic = jnp.sum(offset * offset, axis=0) / (3.0 * spread + EPSILON)
    distance = unwrapped - centre
    radial = jnp.sum(distance * distance, axis=0)
    return (kinetic * live_mask, radial * live_mask)


def local(
    positions, velocities, masses, block_halo, block_shift, block_live, block_count, home_slot
):
    blocks = masses.shape[0]
    halos = home_slot.shape[0]
    owned_count = halos // lax.axis_size(("grp", "dom"))
    valid = jnp.arange(blocks, dtype=jnp.int32) < block_count[0]
    moments, live_mask, unwrapped = block_moments(
        positions, velocities, masses, block_shift, block_live, valid
    )
    slots = home_slot[block_halo]
    domains = lax.axis_size("dom")
    slab_groups = lax.axis_size("grp")
    window = domains * owned_count
    owner = slots // owned_count
    relative = (owner // domains - lax.axis_index("grp")) % slab_groups
    local_column = relative * window + owner % domains * owned_count + slots % owned_count
    table = jnp.zeros((11, 2 * window), jnp.float32).at[:, local_column].add(moments)
    total = lax.psum(jnp.sum(moments[0]), ("grp", "dom"))
    arrived = from_behind(table[:, window:], "grp", 1)
    owned_sums = lax.psum_scatter(
        table[:, :window] + arrived, "dom", scatter_dimension=1, tiled=True
    )
    halo_table = halo_properties(owned_sums, total, halos)
    group_stats = lax.all_gather(halo_table[1:8], "dom", axis=1, tiled=True)
    returned = from_behind(group_stats, "grp", -1)
    stats = jnp.concatenate([group_stats, returned], axis=1)[:, local_column]
    kinetic, radial = particle_outputs(unwrapped, velocities, live_mask, stats)
    return (halo_table, kinetic, radial)


def solution(mesh):
    return jax.shard_map(
        local,
        mesh=mesh,
        in_specs=(
            P(None, ("grp", "dom"), None),
            P(None, ("grp", "dom"), None),
            P(("grp", "dom"), None),
            P(("grp", "dom")),
            P(None, ("grp", "dom")),
            P(("grp", "dom")),
            P(("grp", "dom")),
            P(),
        ),
        out_specs=(P(None, ("grp", "dom")), P(("grp", "dom"), None), P(("grp", "dom"), None)),
        check_vma=False,
    )
```

profile of v0, /device:TPU:0, one launch (start us, length us, event | category | flops | bytes accessed | tf_op | source)
XLA Modules:
  0.0 85.7 jit_solution(2616663069370021129)
XLA Ops:
  7.2 0.0 copy-start
  7.2 0.0 reduce-scatter.2.cloned.1.call-start
  7.2 0.7 convert_element_type.4
  8.6 0.0 copy-start.2
  8.6 1.3 %broadcast_add_fusion = f32[3,128,512]{2,1,0:T(8,128)S(1)} fusion(f32[3,128,512]{2,1,0:T(8,128)} %param.8, f32[3,128]{1,0:T(4,128)S(1)} %convert_element_type.4), kind=kLoop, calls=%fused_computation.10 | loop fusion | flops 196608 | bytes 1574400 | tf_op jit(solution)/shard_map/add | solution.py:29
  9.9 0.0 copy-done.2
  10.0 0.0 copy-start.3
  10.0 0.0 copy-start.4
  10.0 0.0 copy-start.1
  10.0 0.2 multiply_subtract_fusion.2
  10.1 0.8 copy-done.3
  10.9 0.0 copy-done.4
  10.9 0.1 fusion.5
  11.0 0.2 copy-done.1
  11.2 0.4 multiply_reduce_fusion.2
  11.6 0.8 fusion.16
  12.4 0.0 copy-start.5
  12.4 0.1 copy.44
  12.5 0.5 copy-done.5
  13.1 0.0 copy-done
  13.1 1.1 %gather_fusion = s32[128]{0:T(128)S(1)} fusion(s32[4096]{0:T(1024)S(1)} %copy-done, s32[1024]{0:T(1024)S(1)} %pad_clamp_fusion.1), kind=kCustom, calls=%fused_computation | custom fusion | bytes 1536 | tf_op jit(solution)/shard_map/gather | solution.py:73
  14.3 1.1 %scatter_custom_fusion = f32[11,1024]{0,1:T(8,128)S(1)} fusion(s32[128]{0:T(128)S(1)} %fusion.13, f32[128,11]{1,0:T(8,128)S(1)} %copy.44, f32[]{:T(128)} %constant.66.clone.1), kind=kCustom, calls=%fused_computation.17 | custom fusion | flops 1408 | bytes 45060 | tf_op jit(solution)/shard_map/scatter-add | solution.py:80
  15.5 0.1 copy.51
  15.6 3.0 %collective-permute-start = (f32[11,512]{1,0:T(8,128)S(1)}, f32[11,512]{1,0:T(8,128)S(1)}, u32[]{:S(2)}, u32[]{:S(2)}) collective-permute-start(f32[11,512]{1,0:T(8,128)S(1)} %copy.51), channel_id=1, source_target_pairs={{0,4},{4,8},{8,12},{12,16},{16,20},{20,24},{24,28},{28,0},{1,5},{5... | collective-permute-start | bytes 67592 | tf_op jit(solution)/shard_map/ppermute | solution.py:12
  18.6 0.1 copy.50
  18.7 4.8 %collective-permute-done = f32[11,512]{1,0:T(8,128)S(1)} collective-permute-done((f32[11,512]{1,0:T(8,128)S(1)}, f32[11,512]{1,0:T(8,128)S(1)}, u32[]{:S(2)}, u32[]{:S(2)}) %collective-permute-start) | collective-permute-done | bytes 22560 | tf_op jit(solution)/shard_map/ppermute | solution.py:12
  23.5 0.6 add.129
  24.1 0.0 reduce-scatter.2.cloned.1.call-update
  24.2 38.2 %psum.7 = f32[]{:T(128)} all-reduce(f32[]{:T(128)} %get-tuple-element.13), channel_id=1, replica_groups=mesh['grp'=8,'dom'=4] {'grp','dom'}, use_global_device_ids=true, to_apply=%region_9.10 | all-reduce | flops 1 | bytes 8 | tf_op jit(solution)/shard_map/psum | solution.py:81
  62.4 0.0 reduce-scatter.2.cloned.1.call-done
  62.4 0.7 fusion.15
  63.1 0.8 multiply_reduce_fusion.6
  63.9 1.4 %fusion.14 = (f32[1,128]{1,0:T(1,128)S(1)}, f32[1,128]{1,0:T(1,128)S(1)}) fusion(f32[11,128]{1,0:T(8,128)} %reduce-scatter.2.cloned.1.call-done, f32[128]{0:T(128)S(1)} %get-tuple-element.16, f32[]{:T(128)} %psum.7), kind=kLoop, calls=%fused_computation.55 | loop fusion | flops 640 | bytes 2564 | tf_op jit(solution)/shard_map/sub | solution.py:46
  65.3 5.7 %all_gather.3 = f32[7,512]{1,0:T(8,128)S(1)} all-gather(f32[7,128]{1,0:T(8,128)S(1)} %pad_maximum_fusion.1), channel_id=1, replica_groups=mesh['grp'=8,'dom'=4] {'dom'}, dimensions={1}, use_global_device_ids=true | all-gather | bytes 17920 | tf_op jit(solution)/shard_map/all_gather | solution.py:87
  71.1 3.4 %collective-permute-start.1 = (f32[7,512]{1,0:T(8,128)S(1)}, f32[7,512]{1,0:T(8,128)S(1)}, u32[]{:S(2)}, u32[]{:S(2)}) collective-permute-start(f32[7,512]{1,0:T(8,128)S(1)} %all_gather.3), channel_id=1, source_target_pairs={{0,28},{4,0},{8,4},{12,8},{16,12},{20,16},{24,20},{28,24},{1,29},{... | collective-permute-start | bytes 43016 | tf_op jit(solution)/shard_map/ppermute | solution.py:12
  74.4 0.7 divide_subtract_fusion
  75.1 1.2 %concatenate.13 = f32[11,128]{1,0:T(8,128)} concatenate(f32[1,128]{1,0:T(1,128)S(1)} %get-tuple-element.27, f32[3,128]{1,0:T(4,128)S(1)} %get-tuple-element.25, f32[3,128]{1,0:T(4,128)S(1)} %get-tuple-element.17, f32[1,128]{1,0:T(1,128)S(1)} %get-tuple-element.26, f32[3,128]{1,0:T(4,128)S(1)} %divide_subtract_fusion), dimensions={0} | concatenate | bytes 11264 | tf_op jit(solution)/shard_map/concatenate | solution.py:49
  76.3 0.0 collective-permute-done.1
  76.3 0.2 copy.47
  76.6 0.7 gather_fusion.1
  77.2 0.1 fusion.18
  77.3 0.2 fusion.7
  77.5 0.1 copy.48
  77.6 0.1 copy.49
  77.6 0.3 multiply_reduce_fusion
  77.9 0.9 %fusion.4 = (f32[128,512]{1,0:T(8,128)}, f32[128,512]{1,0:T(8,128)}) fusion(f32[128,512]{1,0:T(8,128)S(1)} %get-tuple-element.33, s32[128]{0:T(128)S(1)} %copy-done.4, pred[128]{0:T(512)(128)(4,1)S(1)} %iota_compare_fusion.1, f32[128,512]{1,0:T(8,128)S(1)} %get-tuple-element.34, f32[128]{0:T(128)S(1)} %fusion.7), kind=kLoop, calls=%fused_computation.20 | loop fusion | flops 327680 | bytes 1049728 | tf_op jit(solution)/shard_map/mul | solution.py:60
  (10 shorter events, 0.1 us)
Async XLA Ops:
  7.2 5.9 %copy-start = (s32[4096]{0:T(1024)S(1)}, s32[4096]{0:T(1024)}, u32[]{:S(2)}) copy-start(s32[4096]{0:T(1024)} %param.15) | copy-start | bytes 49156
  7.2 55.2 %reduce-scatter.2.cloned.1.call-start = ((), (), s32[]{:S(2)}) async-start(), calls=%async_computation.1 | async-start | bytes 40960 | tf_op jit(solution)/shard_map/reduce_scatter | solution.py:83
  8.6 1.4 %copy-start.2 = (f32[3,128,512]{2,1,0:T(8,128)S(1)}, f32[3,128,512]{2,1,0:T(8,128)}, u32[]{:S(2)}) copy-start(f32[3,128,512]{2,1,0:T(8,128)} %param.9) | copy-start | bytes 2359300
  10.0 0.9 %copy-start.3 = (f32[128,512]{1,0:T(8,128)S(1)}, f32[128,512]{1,0:T(8,128)}, u32[]{:S(2)}) copy-start(f32[128,512]{1,0:T(8,128)} %param.10) | copy-start | bytes 786436
  10.0 1.0 %copy-start.4 = (s32[128]{0:T(128)S(1)}, s32[128]{0:T(128)}, u32[]{:S(2)}) copy-start(s32[128]{0:T(128)} %param.13) | copy-start | bytes 1540
  10.0 1.2 %copy-start.1 = (f32[3,128,512]{2,1,0:T(8,128)S(1)}, f32[3,128,512]{2,1,0:T(8,128)}, u32[]{:S(2)}) copy-start(f32[3,128,512]{2,1,0:T(8,128)} %param.8) | copy-start | bytes 2359300
  12.4 0.7 copy-start.5
  15.6 7.9 %collective-permute-start = (f32[11,512]{1,0:T(8,128)S(1)}, f32[11,512]{1,0:T(8,128)S(1)}, u32[]{:S(2)}, u32[]{:S(2)}) collective-permute-start(f32[11,512]{1,0:T(8,128)S(1)} %copy.51), channel_id=1, source_target_pairs={{0,4},{4,8},{8,12},{12,16},{16,20},{20,24},{24,28},{28,0},{1,5},{5... | collective-permute-start | bytes 67592 | tf_op jit(solution)/shard_map/ppermute | solution.py:12
  71.1 5.3 %collective-permute-start.1 = (f32[7,512]{1,0:T(8,128)S(1)}, f32[7,512]{1,0:T(8,128)S(1)}, u32[]{:S(2)}, u32[]{:S(2)}) collective-permute-start(f32[7,512]{1,0:T(8,128)S(1)} %all_gather.3), channel_id=1, source_target_pairs={{0,28},{4,0},{8,4},{12,8},{16,12},{20,16},{24,20},{28,24},{1,29},{... | collective-permute-start | bytes 43016 | tf_op jit(solution)/shard_map/ppermute | solution.py:12
Sparse Core Ops, SparseCore 0:
  24.3 18.2 reduce-scatter.1
where the time goes:
time: 86.3 us; the launch traced here: 85.7 us
  blocking collectives  44 us (51%)
  between operations  14.8 us (17%)
  other arithmetic  10.3 us (12%)
  starting transfers between devices  6.41 us (7%)
  local copies, waits for them, and re-layouts  5.38 us (6%)
  waiting for transfers between devices  4.84 us (6%)
    psum x1, blocking collectives, local(): total = lax.psum(jnp.sum(moments[0]), ('grp', 'dom'))  38.2 us
    ppermute x2, starting transfers between devices, from_behind(): lax.ppermute(shard, axis, [(i, (i + by) % devices) for i in range(devices)])  6.37 us
    all_gather x1, blocking collectives, local(): group_stats = lax.all_gather(halo_table[1:8], 'dom', axis=1, tiled=True)  5.74 us
    ppermute x2, waiting for transfers between devices, from_behind(): lax.ppermute(shard, axis, [(i, (i + by) % devices) for i in range(devices)])  4.82 us
    unnamed x14, local copies, waits for them, and re-layouts  1.75 us
  transfers between devices with their start and end apart: 3, of which 1 were waited for; matrix products, arithmetic and copies ran while one was open for 2% of the time, Pallas kernels for 0%

commit v1 on v0

v1 whole, which is shorter than its diff:
```python
import functools

import jax
import jax.numpy as jnp
from jax import lax
from jax.experimental import pallas as pl
from jax.experimental.pallas import tpu as pltpu
from jax.sharding import PartitionSpec as P

EPSILON = 1e-06
LANES = 128
CHUNKS = 4
MOMENTS = 11
AXES = ("grp", "dom")


def rows_to_array(rows, count, width):
    at = lax.broadcasted_iota(jnp.int32, (count, width), 0)
    out = jnp.zeros((count, width), jnp.float32)
    for k, row in enumerate(rows):
        out = jnp.where(at == k, row, out)
    return out


def moments_kernel(
    pos_hbm, vel_hbm, mass_hbm, halo_ref, home_ref, shift_ref, live_ref, count_ref,
    send_ref, pos_ref, vel_ref, side_ref, cols_ref, mass_ref, acc_ref, sems,
):
    blocks, width = mass_ref.shape
    step = blocks // CHUNKS
    copies = []
    for c in range(CHUNKS):
        rows = pl.ds(c * step, step)
        copies.append(
            [
                pltpu.make_async_copy(mass_hbm.at[rows], mass_ref.at[rows], sems.at[0, c]),
                pltpu.make_async_copy(vel_hbm.at[:, rows], vel_ref.at[:, rows], sems.at[1, c]),
                pltpu.make_async_copy(pos_hbm.at[:, rows], pos_ref.at[:, rows], sems.at[2, c]),
            ]
        )
        for copy in copies[c]:
            copy.start()

    halo = halo_ref[...]
    low = lax.broadcasted_iota(jnp.int32, (LANES, blocks), 0) == halo % LANES
    picked = lax.dot_general(
        home_ref[...].astype(jnp.float32), low.astype(jnp.float32), (((1,), (0,)), ((), ())),
        precision=lax.Precision.HIGHEST, preferred_element_type=jnp.float32,
    )
    high = lax.broadcasted_iota(jnp.int32, picked.shape, 0) == halo // LANES
    slot = jnp.sum(jnp.where(high, picked, 0.0), axis=0, keepdims=True)

    at = lax.broadcasted_iota(jnp.int32, (1, blocks), 1)
    live = jnp.where(at < count_ref[0], live_ref[...], 0).astype(jnp.float32)
    shift = shift_ref[...].astype(jnp.float32)
    side = rows_to_array([live, shift[0:1], shift[1:2], shift[2:3], slot], 8, blocks)
    side_ref[...] = side
    cols = jnp.transpose(side)
    cols_ref[...] = cols

    lane = lax.broadcasted_iota(jnp.int32, (8, width), 1).astype(jnp.float32)
    lane_of = lax.broadcasted_iota(jnp.int32, (8, LANES), 1)
    for r in range(0, blocks, 8):
        if r % step == 0:
            for copy in copies[r // step]:
                copy.wait()
        rows = slice(r, r + 8)
        weight = jnp.where(lane < cols[rows, 0:1], mass_ref[rows], 0.0)
        ux, uy, uz = (pos_ref[k, rows] + cols[rows, k + 1 : k + 2] for k in range(3))
        vx, vy, vz = (vel_ref[k, rows] for k in range(3))
        mx, my, mz = weight * vx, weight * vy, weight * vz
        terms = (
            weight, weight * ux, weight * uy, weight * uz, mx, my, mz,
            mx * vx + my * vy + mz * vz,
            uy * mz - uz * my, uz * mx - ux * mz, ux * my - uy * mx,
        )
        acc = jnp.where(lane_of == MOMENTS, cols[rows, 4:5], 0.0)
        for k, term in enumerate(terms):
            acc = jnp.where(lane_of == k, jnp.sum(term, axis=1, keepdims=True), acc)
        acc_ref[rows] = acc

    table = jnp.transpose(acc_ref[...])
    for s in range(send_ref.shape[0]):
        for k in range(3):
            send_ref[s, :, k * blocks : (k + 1) * blocks] = table[4 * k : 4 * k + 4]


def outputs_kernel(
    groups, domains, halos,
    recv_ref, pos_ref, vel_ref, side_ref, cols_ref,
    table_ref, kin_hbm, rad_hbm, kin_ref, rad_ref, sems,
):
    blocks, width = kin_ref.shape
    owned = halos // (groups * domains)
    group, domain = lax.axis_index("grp"), lax.axis_index("dom")

    near = []
    for offset in sorted({o % groups for o in (-1, 0, 1)}):
        first = lax.rem(group + offset, groups) * domains
        for d in range(domains):
            part = recv_ref[first + d]
            near.append(
                jnp.concatenate([part[:, k * blocks : (k + 1) * blocks] for k in range(3)], axis=0)
            )
    base = ((group * domains + domain) * owned).astype(jnp.float32)
    mine = jnp.broadcast_to(cols_ref[:, 4:5], (blocks, LANES))
    own = lax.broadcasted_iota(jnp.int32, (owned, LANES), 0).astype(jnp.float32) + base
    want = jnp.concatenate([mine, own], axis=0)
    same = jnp.concatenate(
        [jnp.where(want == rows[MOMENTS : MOMENTS + 1], 1.0, 0.0).astype(jnp.bfloat16) for rows in near],
        axis=1,
    )
    values = jnp.concatenate(near, axis=1)
    values = jnp.concatenate([values, jnp.zeros((4, values.shape[1]), jnp.float32)], axis=0)
    top = values.astype(jnp.bfloat16)
    rest = values - top.astype(jnp.float32)
    mid = rest.astype(jnp.bfloat16)
    last = (rest - mid.astype(jnp.float32)).astype(jnp.bfloat16)
    sums = lax.dot_general(
        jnp.concatenate([top, mid, last], axis=0), same, (((1,), (1,)), ((), ())),
        preferred_element_type=jnp.float32,
    )
    sums = sums[0:16] + sums[16:32] + sums[32:48]

    heavy = jnp.maximum(sums[0:1], 1.0)
    mean = sums[0:8] / heavy
    cx, cy, cz, dx, dy, dz, energy = (mean[k : k + 1] for k in range(1, 8))
    spread = energy - (dx * dx + dy * dy + dz * dz)

    m = slice(0, blocks)
    side = side_ref[...]
    stats = rows_to_array(
        [
            cx[:, m] - side[1:2], cy[:, m] - side[2:3], cz[:, m] - side[3:4],
            dx[:, m], dy[:, m], dz[:, m], 1.0 / (3.0 * spread[:, m] + EPSILON),
        ],
        8, blocks,
    )
    stats = jnp.transpose(stats)
    cols = cols_ref[...]
    lane = lax.broadcasted_iota(jnp.int32, (8, width), 1).astype(jnp.float32)
    step = blocks // CHUNKS
    copies = []
    for r in range(0, blocks, 8):
        rows = slice(r, r + 8)
        alive = lane < cols[rows, 0:1]
        rx, ry, rz = (pos_ref[k, rows] - stats[rows, k : k + 1] for k in range(3))
        ox, oy, oz = (vel_ref[k, rows] - stats[rows, k + 3 : k + 4] for k in range(3))
        kinetic = (ox * ox + oy * oy + oz * oz) * stats[rows, 6:7]
        kin_ref[rows] = jnp.where(alive, kinetic, 0.0)
        rad_ref[rows] = jnp.where(alive, rx * rx + ry * ry + rz * rz, 0.0)
        if (r + 8) % step == 0:
            c = r // step
            part = pl.ds(c * step, step)
            for k, (src, dst) in enumerate(((kin_ref, kin_hbm), (rad_ref, rad_hbm))):
                copies.append(pltpu.make_async_copy(src.at[part], dst.at[part], sems.at[k, c]))
                copies[-1].start()

    whole = jnp.zeros((4, blocks), jnp.float32)
    for s in range(recv_ref.shape[0]):
        whole = whole + recv_ref[s, :, 0:blocks]
    total = jnp.sum(whole[0:1], axis=1, keepdims=True)
    o = slice(blocks, blocks + owned)
    share = sums[0:1, o] * float(halos) / total
    at = lax.broadcasted_iota(jnp.int32, (8, owned), 0)
    table_ref[0:8] = jnp.where(at == 0, share, jnp.where(at == 7, spread[:, o], mean[:, o]))
    cx, cy, cz, dx, dy, dz = (v[:, o] for v in (cx, cy, cz, dx, dy, dz))
    turn = rows_to_array([cy * dz - cz * dy, cz * dx - cx * dz, cx * dy - cy * dx], 8, owned)
    table_ref[8:11] = (sums[8:16, o] / heavy[:, o] - turn)[0:3]
    for copy in copies:
        copy.wait()


def local(positions, velocities, masses, block_halo, block_shift, block_live, block_count, home_slot):
    blocks, width = masses.shape
    halos = home_slot.shape[0]
    groups, domains = lax.axis_size("grp"), lax.axis_size("dom")
    devices = groups * domains
    anywhere = pl.BlockSpec(memory_space=pl.ANY)
    vmem = pl.BlockSpec(memory_space=pltpu.VMEM)
    send, pos, vel, side, cols = pl.pallas_call(
        moments_kernel,
        out_shape=(
            pltpu.VMEM((devices, 4, 3 * blocks), jnp.float32),
            pltpu.VMEM(positions.shape, jnp.float32),
            pltpu.VMEM(velocities.shape, jnp.float32),
            pltpu.VMEM((8, blocks), jnp.float32),
            pltpu.VMEM((blocks, 8), jnp.float32),
        ),
        in_specs=[anywhere] * 3 + [vmem] * 4 + [pl.BlockSpec(memory_space=pltpu.SMEM)],
        out_specs=(vmem,) * 5,
        scratch_shapes=[
            pltpu.VMEM((blocks, width), jnp.float32),
            pltpu.VMEM((blocks, LANES), jnp.float32),
            pltpu.SemaphoreType.DMA((3, CHUNKS)),
        ],
        compiler_params=pltpu.CompilerParams(vmem_limit_bytes=16 * 1024 * 1024),
        name="moments",
    )(
        positions, velocities, masses, block_halo.reshape(1, blocks),
        home_slot.reshape(halos // LANES, LANES), block_shift, block_live.reshape(1, blocks), block_count,
    )
    recv = lax.all_to_all(send, AXES, 0, 0)
    table, kinetic, radial = pl.pallas_call(
        functools.partial(outputs_kernel, groups, domains, halos),
        out_shape=(
            jax.ShapeDtypeStruct((MOMENTS, halos // devices), jnp.float32),
            jax.ShapeDtypeStruct((blocks, width), jnp.float32),
            jax.ShapeDtypeStruct((blocks, width), jnp.float32),
        ),
        in_specs=[vmem] * 5,
        out_specs=(vmem, anywhere, anywhere),
        scratch_shapes=[
            pltpu.VMEM((blocks, width), jnp.float32),
            pltpu.VMEM((blocks, width), jnp.float32),
            pltpu.SemaphoreType.DMA((2, CHUNKS)),
        ],
        compiler_params=pltpu.CompilerParams(vmem_limit_bytes=16 * 1024 * 1024),
        name="outputs",
    )(recv, pos, vel, side, cols)
    return table, kinetic, radial


def solution(mesh):
    return jax.shard_map(
        local,
        mesh=mesh,
        in_specs=(
            P(None, AXES, None), P(None, AXES, None), P(AXES, None), P(AXES),
            P(None, AXES), P(AXES), P(AXES), P(),
        ),
        out_specs=(P(None, AXES), P(AXES, None), P(AXES, None)),
        check_vma=False,
    )
```

time: 86.3 us -> 27.2 us (0.32)
  blocking collectives: 44 us -> 16.1 us
  between operations: 14.8 us -> 1.32 us
  other arithmetic: 10.3 us -> 0 us
  starting transfers between devices: 6.41 us -> 0 us
  Pallas kernels: 0 us -> 4.84 us
  waiting for transfers between devices: 4.84 us -> 0 us
    psum x1 -> x0, blocking collectives: 38.2 us -> none  [local(): total = lax.psum(jnp.sum(moments[0]), ('grp', 'dom'))]
    all_to_all x0 -> x1, blocking collectives: none -> 16.1 us  [local(): recv = lax.all_to_all(send, AXES, 0, 0)]
    ppermute x2 -> x0, starting transfers between devices: 6.37 us -> none  [from_behind(): lax.ppermute(shard, axis, [(i, (i + by) % devices) for i in range(devices)])]
    all_gather x1 -> x0, blocking collectives: 5.74 us -> none  [local(): group_stats = lax.all_gather(halo_table[1:8], 'dom', axis=1, tiled=True)]
    pallas_call x0 -> x2, Pallas kernels: none -> 4.84 us  [the longest x1 2.73 us: local(): pl.pallas_call(moments_kernel, out_shape=(pltpu.VMEM((devices, 4, 3 * blo...]
    ppermute x2 -> x0, waiting for transfers between devices: 4.82 us -> none  [from_behind(): lax.ppermute(shard, axis, [(i, (i + by) % devices) for i in range(devices)])]
    unnamed x14, local copies, waits for them, and re-layouts: 1.75 us -> 4.6 us
    sub x4 -> x0, other arithmetic: 2.27 us -> none  [the longest x1 1.41 us: halo_properties(): spread = sums[7] / heavy - jnp.sum(drift * drift, axis=0)]
  transfers between devices with their start and end apart: 3 -> 0, of which waited for: 1 -> 0; matrix products, arithmetic and copies ran while one was open for 2% -> 0% of each run, Pallas kernels for 0% -> 0%
where the time goes in v1:
time: 27.2 us; the launch traced here: 26.8 us
  blocking collectives  16.1 us (59%)
  Pallas kernels  4.84 us (18%)
  local copies, waits for them, and re-layouts  4.6 us (17%)
  between operations  1.32 us (5%)
    all_to_all x1, blocking collectives, local(): recv = lax.all_to_all(send, AXES, 0, 0)  16.1 us
    unnamed x14, local copies, waits for them, and re-layouts  4.6 us
    pallas_call x1, Pallas kernels, local(): pl.pallas_call(moments_kernel, out_shape=(pltpu.VMEM((devices, 4, 3 * blo...  2.73 us
    pallas_call x1, Pallas kernels, local(): pl.pallas_call(functools.partial(outputs_kernel, groups, domains, halos),...  2.11 us

profile of v1, /device:TPU:0, one launch (start us, length us, event | category | flops | bytes accessed | tf_op | source)
XLA Modules:
  0.0 26.8 jit_solution(5355011137564490356)
XLA Ops:
  1.3 0.0 copy-start.4
  1.3 0.0 copy-start.5
  1.3 0.0 copy-start.6
  1.3 0.7 %copy-done.4 = s32[3,128]{1,0:T(4,128)S(1)} copy-done((s32[3,128]{1,0:T(4,128)S(1)}, s32[3,128]{1,0:T(4,128)}, u32[]{:S(2)}) %copy-start.4) | copy-done | bytes 1560
  2.0 0.0 copy-done.5
  2.0 0.0 copy-done.6
  2.0 0.0 copy-start
  2.0 1.1 %copy-done = f32[3,128,512]{2,1,0:T(8,128)S(1)} copy-done((f32[3,128,512]{2,1,0:T(8,128)S(1)}, f32[3,128,512]{2,1,0:T(8,128)}, u32[]{:S(2)}) %copy-start) | copy-done | bytes 786456
  3.1 0.0 copy-start.1
  3.1 1.1 %copy-done.1 = f32[3,128,512]{2,1,0:T(8,128)S(1)} copy-done((f32[3,128,512]{2,1,0:T(8,128)S(1)}, f32[3,128,512]{2,1,0:T(8,128)}, u32[]{:S(2)}) %copy-start.1) | copy-done | bytes 786456
  4.2 0.0 copy-start.2
  4.2 0.9 %copy-done.2 = f32[128,512]{1,0:T(8,128)S(1)} copy-done((f32[128,512]{1,0:T(8,128)S(1)}, f32[128,512]{1,0:T(8,128)}, u32[]{:S(2)}) %copy-start.2) | copy-done | bytes 262168
  5.2 0.0 copy-start.3
  5.2 0.7 %copy-done.3 = s32[4096]{0:T(1024)S(1)} copy-done((s32[4096]{0:T(1024)S(1)}, s32[4096]{0:T(1024)}, u32[]{:S(2)}) %copy-start.3) | copy-done | bytes 16408
  5.9 2.7 %moments.1 = (f32[32,4,384]{2,1,0:T(4,128)S(1)}, f32[3,128,512]{2,1,0:T(8,128)S(1)}, f32[3,128,512]{2,1,0:T(8,128)S(1)}, f32[8,128]{1,0:T(8,128)S(1)}, f32[128,8]{1,0:T(8,128)S(1)}) custom-call(f32[3,128,512]{2,1,0:T(8,128)S(1)} %copy-done, f32[3,128,512]{2,1,0:T(8,128)S(1)} %copy-done.1, f32[128,512]{1,0:T(8,128)S(1)} %copy-done.2, s32[1,128]{1,0:T(1,128)S(1)} %bitcast.4, ...), custom_call_target="tpu_custom_call" | custom-call | tf_op jit(solution)/shard_map/moments/pallas_call | solution.py:181
  8.6 16.1 %all_to_all.5.recv_ref = f32[32,4,384]{2,1,0:T(4,128)S(1)} all-to-all(f32[32,4,384]{2,1,0:T(4,128)S(1)} %get-tuple-element.8), channel_id=1, replica_groups=mesh['grp'=8,'dom'=4] {'grp','dom'}, dimensions={0} | all-to-all | bytes 393216 | tf_op jit(solution)/shard_map/all_to_all | solution.py:203
  24.7 2.1 %outputs.1 = (f32[11,128]{1,0:T(8,128)}, f32[128,512]{1,0:T(8,128)}, f32[128,512]{1,0:T(8,128)}) custom-call(f32[32,4,384]{2,1,0:T(4,128)S(1)} %all_to_all.5.recv_ref, f32[3,128,512]{2,1,0:T(8,128)S(1)} %get-tuple-element.9.pos_ref, f32[3,128,512]{2,1,0:T(8,128)S(1)} %get-tuple-element.10.vel_ref, f32[8,128]{1,0:T(8,128)S(1)} %get-tuple-element.11.side_ref, ...), custom_call_target="tpu_custom_call" | custom-call | tf_op jit(solution)/shard_map/outputs/pallas_call | solution.py:204
Async XLA Ops:
  1.3 0.7 %copy-start.4 = (s32[3,128]{1,0:T(4,128)S(1)}, s32[3,128]{1,0:T(4,128)}, u32[]{:S(2)}) copy-start(s32[3,128]{1,0:T(4,128)} %shift_ref.1) | copy-start | bytes 4612
  1.3 0.7 %copy-start.5 = (s32[128]{0:T(128)S(1)}, s32[128]{0:T(128)}, u32[]{:S(2)}) copy-start(s32[128]{0:T(128)} %param.11) | copy-start | bytes 1540
  1.3 0.7 %copy-start.6 = (s32[128]{0:T(128)S(1)}, s32[128]{0:T(128)}, u32[]{:S(2)}) copy-start(s32[128]{0:T(128)} %param.13) | copy-start | bytes 1540
  2.0 1.1 %copy-start = (f32[3,128,512]{2,1,0:T(8,128)S(1)}, f32[3,128,512]{2,1,0:T(8,128)}, u32[]{:S(2)}) copy-start(f32[3,128,512]{2,1,0:T(8,128)} %pos_hbm.1) | copy-start | bytes 2359300
  3.1 1.1 %copy-start.1 = (f32[3,128,512]{2,1,0:T(8,128)S(1)}, f32[3,128,512]{2,1,0:T(8,128)}, u32[]{:S(2)}) copy-start(f32[3,128,512]{2,1,0:T(8,128)} %vel_hbm.1) | copy-start | bytes 2359300
  4.2 0.9 %copy-start.2 = (f32[128,512]{1,0:T(8,128)S(1)}, f32[128,512]{1,0:T(8,128)}, u32[]{:S(2)}) copy-start(f32[128,512]{1,0:T(8,128)} %mass_hbm.1) | copy-start | bytes 786436
  5.2 0.7 %copy-start.3 = (s32[4096]{0:T(1024)S(1)}, s32[4096]{0:T(1024)}, u32[]{:S(2)}) copy-start(s32[4096]{0:T(1024)} %param.15) | copy-start | bytes 49156

commit v2 on v1

--- a/solution.py
+++ b/solution.py
@@ -23,11 +23,23 @@
 
 
 def moments_kernel(
-    pos_hbm, vel_hbm, mass_hbm, halo_ref, home_ref, shift_ref, live_ref, count_ref,
-    send_ref, pos_ref, vel_ref, side_ref, cols_ref, mass_ref, acc_ref, sems,
+    pos_hbm, vel_hbm, mass_hbm, halo_hbm, home_hbm, shift_hbm, live_hbm, count_hbm,
+    send_ref, pos_ref, vel_ref, side_ref, cols_ref, mass_ref, acc_ref,
+    halo_ref, home_ref, shift_ref, live_ref, count_ref, sems, small_sems,
 ):
     blocks, width = mass_ref.shape
     step = blocks // CHUNKS
+    small = [
+        pltpu.make_async_copy(src, dst, small_sems.at[k])
+        for k, (src, dst) in enumerate(
+            (
+                (count_hbm, count_ref), (halo_hbm, halo_ref), (home_hbm, home_ref),
+                (shift_hbm, shift_ref), (live_hbm, live_ref),
+            )
+        )
+    ]
+    for copy in small:
+        copy.start()
     copies = []
     for c in range(CHUNKS):
         rows = pl.ds(c * step, step)
@@ -40,6 +52,9 @@
         )
         for copy in copies[c]:
             copy.start()
+
+    for copy in small:
+        copy.wait()
 
     halo = halo_ref[...]
     low = lax.broadcasted_iota(jnp.int32, (LANES, blocks), 0) == halo % LANES
@@ -177,7 +192,9 @@
     groups, domains = lax.axis_size("grp"), lax.axis_size("dom")
     devices = groups * domains
     anywhere = pl.BlockSpec(memory_space=pl.ANY)
+    hbm = pl.BlockSpec(memory_space=pltpu.HBM)
     vmem = pl.BlockSpec(memory_space=pltpu.VMEM)
+    held = functools.partial(pltpu.with_memory_space_constraint, memory_space=pltpu.HBM)
     send, pos, vel, side, cols = pl.pallas_call(
         moments_kernel,
         out_shape=(
@@ -187,18 +204,30 @@
             pltpu.VMEM((8, blocks), jnp.float32),
             pltpu.VMEM((blocks, 8), jnp.float32),
         ),
-        in_specs=[anywhere] * 3 + [vmem] * 4 + [pl.BlockSpec(memory_space=pltpu.SMEM)],
+        in_specs=[hbm] * 7 + [anywhere],
         out_specs=(vmem,) * 5,
         scratch_shapes=[
             pltpu.VMEM((blocks, width), jnp.float32),
             pltpu.VMEM((blocks, LANES), jnp.float32),
+            pltpu.VMEM((1, blocks), jnp.int32),
+            pltpu.VMEM((halos // LANES, LANES), jnp.int32),
+            pltpu.VMEM((3, blocks), jnp.int32),
+            pltpu.VMEM((1, blocks), jnp.int32),
+            pltpu.SMEM((1,), jnp.int32),
             pltpu.SemaphoreType.DMA((3, CHUNKS)),
+            pltpu.SemaphoreType.DMA((5,)),
         ],
         compiler_params=pltpu.CompilerParams(vmem_limit_bytes=16 * 1024 * 1024),
         name="moments",
     )(
-        positions, velocities, masses, block_halo.reshape(1, blocks),
-        home_slot.reshape(halos // LANES, LANES), block_shift, block_live.reshape(1, blocks), block_count,
+        *map(
+            held,
+            (
+                positions, velocities, masses, block_halo.reshape(1, blocks),
+                home_slot.reshape(halos // LANES, LANES), block_shift, block_live.reshape(1, blocks),
+            ),
+        ),
+        block_count,
     )
     recv = lax.all_to_all(send, AXES, 0, 0)
     table, kinetic, radial = pl.pallas_call(

time: 27.2 us -> 22.7 us (0.83)
  local copies, waits for them, and re-layouts: 4.6 us -> 0 us
  Pallas kernels: 4.84 us -> 5.17 us
    unnamed x14 -> x0, local copies, waits for them, and re-layouts: 4.6 us -> none
    pallas_call x1, Pallas kernels: 2.73 us -> 3.05 us  [local(): pl.pallas_call(moments_kernel, out_shape=(pltpu.VMEM((devices, 4, 3 * blo...]
where the time goes in v2:
time: 22.7 us; the launch traced here: 22.5 us
  blocking collectives  16.1 us (71%)
  Pallas kernels  5.17 us (23%)
  between operations  1.29 us (6%)
    all_to_all x1, blocking collectives, local(): recv = lax.all_to_all(send, AXES, 0, 0)  16.1 us
    pallas_call x1, Pallas kernels, local(): pl.pallas_call(moments_kernel, out_shape=(pltpu.VMEM((devices, 4, 3 * blo...  3.05 us
    pallas_call x1, Pallas kernels, local(): pl.pallas_call(functools.partial(outputs_kernel, groups, domains, halos),...  2.12 us

profile of v2, /device:TPU:0, one launch (start us, length us, event | category | flops | bytes accessed | tf_op | source)
XLA Modules:
  0.0 22.5 jit_solution(14405042893977220682)
XLA Ops:
  1.3 3.0 %moments.1 = (f32[32,4,384]{2,1,0:T(4,128)S(1)}, f32[3,128,512]{2,1,0:T(8,128)S(1)}, f32[3,128,512]{2,1,0:T(8,128)S(1)}, f32[8,128]{1,0:T(8,128)S(1)}, f32[128,8]{1,0:T(8,128)S(1)}) custom-call(f32[3,128,512]{2,1,0:T(8,128)} %pos_hbm.1, f32[3,128,512]{2,1,0:T(8,128)} %vel_hbm.1, f32[128,512]{1,0:T(8,128)} %mass_hbm.1, s32[1,128]{1,0:T(1,128)} %bitcast.4, ...), custom_call_target="tpu_custom_call" | custom-call | tf_op jit(solution)/shard_map/moments/pallas_call | solution.py:198
  4.3 16.1 %all_to_all.5.recv_ref = f32[32,4,384]{2,1,0:T(4,128)S(1)} all-to-all(f32[32,4,384]{2,1,0:T(4,128)S(1)} %get-tuple-element.8), channel_id=1, replica_groups=mesh['grp'=8,'dom'=4] {'grp','dom'}, dimensions={0} | all-to-all | bytes 393216 | tf_op jit(solution)/shard_map/all_to_all | solution.py:232
  20.4 2.1 %outputs.1 = (f32[11,128]{1,0:T(8,128)}, f32[128,512]{1,0:T(8,128)}, f32[128,512]{1,0:T(8,128)}) custom-call(f32[32,4,384]{2,1,0:T(4,128)S(1)} %all_to_all.5.recv_ref, f32[3,128,512]{2,1,0:T(8,128)S(1)} %get-tuple-element.9.pos_ref, f32[3,128,512]{2,1,0:T(8,128)S(1)} %get-tuple-element.10.vel_ref, f32[8,128]{1,0:T(8,128)S(1)} %get-tuple-element.11.side_ref, ...), custom_call_target="tpu_custom_call" | custom-call | tf_op jit(solution)/shard_map/outputs/pallas_call | solution.py:233

commit v3 on v2

v3 whole, which is shorter than its diff:
```python
import functools

import jax
import jax.numpy as jnp
from jax import lax
from jax.experimental import pallas as pl
from jax.experimental.pallas import tpu as pltpu
from jax.sharding import PartitionSpec as P

EPSILON = 1e-06
LANES = 128
OUT_CHUNKS = 2
MOMENTS = 11
AXES = ("grp", "dom")


def rows_to_array(rows, count, width):
    at = lax.broadcasted_iota(jnp.int32, (count, width), 0)
    out = jnp.zeros((count, width), jnp.float32)
    for k, row in enumerate(rows):
        out = jnp.where(at == k, row, out)
    return out


def moments_kernel(
    pos_hbm, vel_hbm, mass_hbm, halo_hbm, home_hbm, shift_hbm, live_hbm, count_ref,
    send_ref, pos_ref, vel_ref, side_ref, cols_ref, mass_ref, part_ref,
    halo_ref, home_ref, shift_ref, live_ref, sems, small_sems,
):
    blocks, width = mass_ref.shape
    small = [
        pltpu.make_async_copy(src, dst, small_sems.at[k])
        for k, (src, dst) in enumerate(
            (
                (halo_hbm, halo_ref), (home_hbm, home_ref), (shift_hbm, shift_ref), (live_hbm, live_ref),
            )
        )
    ]
    large = [
        pltpu.make_async_copy(src, dst, sems.at[k])
        for k, (src, dst) in enumerate(
            ((mass_hbm, mass_ref), (vel_hbm, vel_ref), (pos_hbm, pos_ref))
        )
    ]
    for copy in small + large:
        copy.start()

    for copy in small:
        copy.wait()

    halo = halo_ref[...]
    low = lax.broadcasted_iota(jnp.int32, (LANES, blocks), 0) == halo % LANES
    picked = lax.dot_general(
        home_ref[...].astype(jnp.float32), low.astype(jnp.float32), (((1,), (0,)), ((), ())),
        precision=lax.Precision.HIGHEST, preferred_element_type=jnp.float32,
    )
    high = lax.broadcasted_iota(jnp.int32, picked.shape, 0) == halo // LANES
    slot = jnp.sum(jnp.where(high, picked, 0.0), axis=0, keepdims=True)

    at = lax.broadcasted_iota(jnp.int32, (1, blocks), 1)
    live = jnp.where(at < count_ref[0], live_ref[...], 0).astype(jnp.float32)
    shift = shift_ref[...].astype(jnp.float32)
    sx, sy, sz = shift[0:1], shift[1:2], shift[2:3]
    side_ref[...] = rows_to_array([live, sx, sy, sz, slot], 8, blocks)
    cols_ref[0] = jnp.transpose(jnp.broadcast_to(live, (LANES, blocks)))
    cols_ref[1] = jnp.transpose(jnp.broadcast_to(slot, (LANES, blocks)))

    lane = lax.broadcasted_iota(jnp.int32, (8, width), 1).astype(jnp.float32)

    for copy in large:
        copy.wait()
    for r in range(0, blocks, 8):
        rows = slice(r, r + 8)
        edge = cols_ref[0, rows]
        edge = jnp.concatenate([edge] * (width // LANES), axis=1)
        weight = jnp.where(lane < edge, mass_ref[rows], 0.0)
        px, py, pz = (pos_ref[k, rows] for k in range(3))
        vx, vy, vz = (vel_ref[k, rows] for k in range(3))
        mx, my, mz = weight * vx, weight * vy, weight * vz
        terms = (
            weight, weight * px, weight * py, weight * pz, mx, my, mz,
            mx * vx + my * vy + mz * vz,
            py * mz - pz * my, pz * mx - px * mz, px * my - py * mx,
        )
        for k, term in enumerate(terms):
            part = term[:, 0:LANES]
            for n in range(LANES, width, LANES):
                part = part + term[:, n : n + LANES]
            part_ref[k, rows] = part

    raw = [jnp.sum(jnp.transpose(part_ref[k]), axis=0, keepdims=True) for k in range(MOMENTS)]
    w, rx, ry, rz, mx, my, mz, energy, ax, ay, az = raw
    table = rows_to_array(
        [
            w, rx + w * sx, ry + w * sy, rz + w * sz, mx, my, mz, energy,
            ax + (sy * mz - sz * my), ay + (sz * mx - sx * mz), az + (sx * my - sy * mx), slot,
        ],
        16, blocks,
    )
    for s in range(send_ref.shape[0]):
        for k in range(3):
            send_ref[s, :, k * blocks : (k + 1) * blocks] = table[4 * k : 4 * k + 4]


def outputs_kernel(
    groups, domains, halos,
    recv_ref, pos_ref, vel_ref, side_ref, cols_ref,
    table_hbm, kin_hbm, rad_hbm, table_ref, kin_ref, rad_ref, stats_ref, sems, table_sem,
):
    blocks, width = kin_ref.shape
    owned = halos // (groups * domains)
    group, domain = lax.axis_index("grp"), lax.axis_index("dom")

    near = []
    for offset in sorted({o % groups for o in (-1, 0, 1)}):
        source = lax.rem(group + offset, groups)
        for d in range(domains):
            part = recv_ref[d * groups + source]
            near.append(
                jnp.concatenate([part[:, k * blocks : (k + 1) * blocks] for k in range(3)], axis=0)
            )
    base = ((group * domains + domain) * owned).astype(jnp.float32)
    mine = cols_ref[1]
    own = lax.broadcasted_iota(jnp.int32, (owned, LANES), 0).astype(jnp.float32) + base
    want = jnp.concatenate([mine, own], axis=0)
    same = jnp.concatenate(
        [jnp.where(want == rows[MOMENTS : MOMENTS + 1], 1.0, 0.0).astype(jnp.bfloat16) for rows in near],
        axis=1,
    )
    values = jnp.concatenate(near, axis=1)
    values = jnp.concatenate([values, jnp.zeros((4, values.shape[1]), jnp.float32)], axis=0)
    top = values.astype(jnp.bfloat16)
    rest = values - top.astype(jnp.float32)
    mid = rest.astype(jnp.bfloat16)
    last = (rest - mid.astype(jnp.float32)).astype(jnp.bfloat16)
    sums = lax.dot_general(
        jnp.concatenate([top, mid, last], axis=0), same, (((1,), (1,)), ((), ())),
        preferred_element_type=jnp.float32,
    )
    sums = sums[0:16] + sums[16:32] + sums[32:48]

    heavy = jnp.maximum(sums[0:1], 1.0)
    mean = sums[0:8] / heavy
    cx, cy, cz, dx, dy, dz, energy = (mean[k : k + 1] for k in range(1, 8))
    spread = energy - (dx * dx + dy * dy + dz * dz)

    m = slice(0, blocks)
    side = side_ref[...]
    stats = rows_to_array(
        [
            cx[:, m] - side[1:2], cy[:, m] - side[2:3], cz[:, m] - side[3:4],
            dx[:, m], dy[:, m], dz[:, m], 1.0 / (3.0 * spread[:, m] + EPSILON),
        ],
        8, blocks,
    )
    stats_ref[...] = jnp.transpose(stats)

    whole = jnp.zeros((4, blocks), jnp.float32)
    for s in range(recv_ref.shape[0]):
        whole = whole + recv_ref[s, :, 0:blocks]
    total = jnp.sum(whole[0:1], axis=1, keepdims=True)
    o = slice(blocks, blocks + owned)
    share = sums[0:1, o] * float(halos) / total
    at = lax.broadcasted_iota(jnp.int32, (8, owned), 0)
    table_ref[0:8] = jnp.where(at == 0, share, jnp.where(at == 7, spread[:, o], mean[:, o]))
    cx, cy, cz, dx, dy, dz = (v[:, o] for v in (cx, cy, cz, dx, dy, dz))
    turn = rows_to_array([cy * dz - cz * dy, cz * dx - cx * dz, cx * dy - cy * dx], 8, owned)
    table_ref[8:11] = (sums[8:16, o] / heavy[:, o] - turn)[0:3]
    table_copy = pltpu.make_async_copy(table_ref, table_hbm, table_sem)
    table_copy.start()

    lane = lax.broadcasted_iota(jnp.int32, (8, width), 1).astype(jnp.float32)
    step = blocks // OUT_CHUNKS

    def leaving(c):
        part = pl.ds(pl.multiple_of(c * step, step), step)
        return (
            pltpu.make_async_copy(kin_ref.at[part], kin_hbm.at[part], sems.at[0, c]),
            pltpu.make_async_copy(rad_ref.at[part], rad_hbm.at[part], sems.at[1, c]),
        )

    @pl.loop(0, OUT_CHUNKS)
    def _(c):
        for r in range(0, step, 8):
            rows = pl.ds(pl.multiple_of(c * step + r, 8), 8)
            stat = stats_ref[rows]
            alive = lane < jnp.concatenate([cols_ref[0, rows]] * (width // LANES), axis=1)
            rx, ry, rz = (pos_ref[k, rows] - stat[:, k : k + 1] for k in range(3))
            ox, oy, oz = (vel_ref[k, rows] - stat[:, k + 3 : k + 4] for k in range(3))
            kinetic = (ox * ox + oy * oy + oz * oz) * stat[:, 6:7]
            kin_ref[rows] = jnp.where(alive, kinetic, 0.0)
            rad_ref[rows] = jnp.where(alive, rx * rx + ry * ry + rz * rz, 0.0)
        for copy in leaving(c):
            copy.start()

    for c in range(OUT_CHUNKS):
        for copy in leaving(c):
            copy.wait()
    table_copy.wait()


def local(positions, velocities, masses, block_halo, block_shift, block_live, block_count, home_slot):
    blocks, width = masses.shape
    halos = home_slot.shape[0]
    groups, domains = lax.axis_size("grp"), lax.axis_size("dom")
    devices = groups * domains
    anywhere = pl.BlockSpec(memory_space=pl.ANY)
    hbm = pl.BlockSpec(memory_space=pltpu.HBM)
    vmem = pl.BlockSpec(memory_space=pltpu.VMEM)
    held = functools.partial(pltpu.with_memory_space_constraint, memory_space=pltpu.HBM)
    send, pos, vel, side, cols = pl.pallas_call(
        moments_kernel,
        out_shape=(
            pltpu.VMEM((devices, 4, 3 * blocks), jnp.float32),
            pltpu.VMEM(positions.shape, jnp.float32),
            pltpu.VMEM(velocities.shape, jnp.float32),
            pltpu.VMEM((8, blocks), jnp.float32),
            pltpu.VMEM((2, blocks, LANES), jnp.float32),
        ),
        in_specs=[hbm] * 7 + [pl.BlockSpec(memory_space=pltpu.SMEM)],
        out_specs=(vmem,) * 5,
        scratch_shapes=[
            pltpu.VMEM((blocks, width), jnp.float32),
            pltpu.VMEM((MOMENTS, blocks, LANES), jnp.float32),
            pltpu.VMEM((1, blocks), jnp.int32),
            pltpu.VMEM((halos // LANES, LANES), jnp.int32),
            pltpu.VMEM((3, blocks), jnp.int32),
            pltpu.VMEM((1, blocks), jnp.int32),
            pltpu.SemaphoreType.DMA((3,)),
            pltpu.SemaphoreType.DMA((4,)),
        ],
        compiler_params=pltpu.CompilerParams(vmem_limit_bytes=16 * 1024 * 1024),
        name="moments",
    )(
        *map(
            held,
            (
                positions, velocities, masses, block_halo.reshape(1, blocks),
                home_slot.reshape(halos // LANES, LANES), block_shift, block_live.reshape(1, blocks),
            ),
        ),
        block_count,
    )
    recv = lax.all_to_all(send, AXES[::-1], 0, 0)
    table, kinetic, radial = pl.pallas_call(
        functools.partial(outputs_kernel, groups, domains, halos),
        out_shape=(
            jax.ShapeDtypeStruct((MOMENTS, halos // devices), jnp.float32),
            jax.ShapeDtypeStruct((blocks, width), jnp.float32),
            jax.ShapeDtypeStruct((blocks, width), jnp.float32),
        ),
        in_specs=[vmem] * 5,
        out_specs=(anywhere,) * 3,
        scratch_shapes=[
            pltpu.VMEM((MOMENTS, halos // devices), jnp.float32),
            pltpu.VMEM((blocks, width), jnp.float32),
            pltpu.VMEM((blocks, width), jnp.float32),
            pltpu.VMEM((blocks, 8), jnp.float32),
            pltpu.SemaphoreType.DMA((2, OUT_CHUNKS)),
            pltpu.SemaphoreType.DMA,
        ],
        compiler_params=pltpu.CompilerParams(vmem_limit_bytes=16 * 1024 * 1024),
        name="outputs",
    )(recv, pos, vel, side, cols)
    return table, kinetic, radial


def solution(mesh):
    return jax.shard_map(
        local,
        mesh=mesh,
        in_specs=(
            P(None, AXES, None), P(None, AXES, None), P(AXES, None), P(AXES),
            P(None, AXES), P(AXES), P(AXES), P(),
        ),
        out_specs=(P(None, AXES), P(AXES, None), P(AXES, None)),
        check_vma=False,
    )
```

time: 22.7 us -> 20.4 us (0.90)
  Pallas kernels: 5.17 us -> 3.58 us
  blocking collectives: 16.1 us -> 15.4 us
    pallas_call x1, Pallas kernels: 3.05 us -> 2.02 us  [local(): pl.pallas_call(moments_kernel, out_shape=(pltpu.VMEM((devices, 4, 3 * blo...]
    all_to_all x1, blocking collectives: 16.1 us -> 15.4 us  [local(): recv = lax.all_to_all(send, AXES[::-1], 0, 0)]
    pallas_call x1, Pallas kernels: 2.12 us -> 1.56 us  [local(): pl.pallas_call(functools.partial(outputs_kernel, groups, domains, halos),...]
where the time goes in v3:
time: 20.4 us; the launch traced here: 20.3 us
  blocking collectives  15.4 us (75%)
  Pallas kernels  3.58 us (18%)
  between operations  1.29 us (6%)
    all_to_all x1, blocking collectives, local(): recv = lax.all_to_all(send, AXES[::-1], 0, 0)  15.4 us
    pallas_call x1, Pallas kernels, local(): pl.pallas_call(moments_kernel, out_shape=(pltpu.VMEM((devices, 4, 3 * blo...  2.02 us
    pallas_call x1, Pallas kernels, local(): pl.pallas_call(functools.partial(outputs_kernel, groups, domains, halos),...  1.56 us

profile of v3, /device:TPU:0, one launch (start us, length us, event | category | flops | bytes accessed | tf_op | source)
XLA Modules:
  0.0 20.3 jit_solution(10510902132915302400)
XLA Ops:
  1.3 2.0 %moments.1 = (f32[32,4,384]{2,1,0:T(4,128)S(1)}, f32[3,128,512]{2,1,0:T(8,128)S(1)}, f32[3,128,512]{2,1,0:T(8,128)S(1)}, f32[8,128]{1,0:T(8,128)S(1)}, f32[2,128,128]{2,1,0:T(8,128)S(1)}) custom-call(f32[3,128,512]{2,1,0:T(8,128)} %pos_hbm.1, f32[3,128,512]{2,1,0:T(8,128)} %vel_hbm.1, f32[128,512]{1,0:T(8,128)} %mass_hbm.1, s32[1,128]{1,0:T(1,128)} %bitcast.4, ...), custom_call_target="tpu_custom_call" | custom-call | tf_op jit(solution)/shard_map/moments/pallas_call | solution.py:211
  3.3 15.4 %all_to_all.5.recv_ref = f32[32,4,384]{2,1,0:T(4,128)S(1)} all-to-all(f32[32,4,384]{2,1,0:T(4,128)S(1)} %get-tuple-element.8), channel_id=1, replica_groups=mesh['grp'=8,'dom'=4] {'dom','grp'}, dimensions={0} | all-to-all | bytes 393216 | tf_op jit(solution)/shard_map/all_to_all | solution.py:244
  18.7 1.6 %outputs.1 = (f32[11,128]{1,0:T(8,128)}, f32[128,512]{1,0:T(8,128)}, f32[128,512]{1,0:T(8,128)}) custom-call(f32[32,4,384]{2,1,0:T(4,128)S(1)} %all_to_all.5.recv_ref, f32[3,128,512]{2,1,0:T(8,128)S(1)} %get-tuple-element.9.pos_ref, f32[3,128,512]{2,1,0:T(8,128)S(1)} %get-tuple-element.10.vel_ref, f32[8,128]{1,0:T(8,128)S(1)} %get-tuple-element.11.side_ref, ...), custom_call_target="tpu_custom_call" | custom-call | tf_op jit(solution)/shard_map/outputs/pallas_call | solution.py:245

commit v4 on v3

--- a/solution.py
+++ b/solution.py
@@ -10,6 +10,8 @@
 EPSILON = 1e-06
 LANES = 128
 OUT_CHUNKS = 2
+FLOPS = 1000000000
+BYTES = 10000000
 MOMENTS = 11
 AXES = ("grp", "dom")
 
@@ -22,30 +24,22 @@
     return out
 
 
-def moments_kernel(
-    pos_hbm, vel_hbm, mass_hbm, halo_hbm, home_hbm, shift_hbm, live_hbm, count_ref,
-    send_ref, pos_ref, vel_ref, side_ref, cols_ref, mass_ref, part_ref,
-    halo_ref, home_ref, shift_ref, live_ref, sems, small_sems,
+def blocks_kernel(
+    halo_hbm, home_hbm, shift_hbm, live_hbm, count_ref,
+    side_ref, cols_ref, halo_ref, home_ref, shift_ref, live_ref, sems,
 ):
-    blocks, width = mass_ref.shape
-    small = [
-        pltpu.make_async_copy(src, dst, small_sems.at[k])
+    blocks = side_ref.shape[1]
+    copies = [
+        pltpu.make_async_copy(src, dst, sems.at[k])
         for k, (src, dst) in enumerate(
             (
                 (halo_hbm, halo_ref), (home_hbm, home_ref), (shift_hbm, shift_ref), (live_hbm, live_ref),
             )
         )
     ]
-    large = [
-        pltpu.make_async_copy(src, dst, sems.at[k])
-        for k, (src, dst) in enumerate(
-            ((mass_hbm, mass_ref), (vel_hbm, vel_ref), (pos_hbm, pos_ref))
-        )
-    ]
-    for copy in small + large:
+    for copy in copies:
         copy.start()
-
-    for copy in small:
+    for copy in copies:
         copy.wait()
 
     halo = halo_ref[...]
@@ -60,15 +54,16 @@
     at = lax.broadcasted_iota(jnp.int32, (1, blocks), 1)
     live = jnp.where(at < count_ref[0], live_ref[...], 0).astype(jnp.float32)
     shift = shift_ref[...].astype(jnp.float32)
-    sx, sy, sz = shift[0:1], shift[1:2], shift[2:3]
-    side_ref[...] = rows_to_array([live, sx, sy, sz, slot], 8, blocks)
+    side_ref[...] = rows_to_array([live, shift[0:1], shift[1:2], shift[2:3], slot], 8, blocks)
     cols_ref[0] = jnp.transpose(jnp.broadcast_to(live, (LANES, blocks)))
     cols_ref[1] = jnp.transpose(jnp.broadcast_to(slot, (LANES, blocks)))
 
+
+def moments_kernel(pos_ref, vel_ref, mass_ref, side_ref, cols_ref, send_ref, part_ref):
+    blocks, width = mass_ref.shape
+    side = side_ref[...]
+    sx, sy, sz, slot = (side[k : k + 1] for k in range(1, 5))
     lane = lax.broadcasted_iota(jnp.int32, (8, width), 1).astype(jnp.float32)
-
-    for copy in large:
-        copy.wait()
     for r in range(0, blocks, 8):
         rows = slice(r, r + 8)
         edge = cols_ref[0, rows]
@@ -207,40 +202,45 @@
     anywhere = pl.BlockSpec(memory_space=pl.ANY)
     hbm = pl.BlockSpec(memory_space=pltpu.HBM)
     vmem = pl.BlockSpec(memory_space=pltpu.VMEM)
+    smem = pl.BlockSpec(memory_space=pltpu.SMEM)
     held = functools.partial(pltpu.with_memory_space_constraint, memory_space=pltpu.HBM)
-    send, pos, vel, side, cols = pl.pallas_call(
-        moments_kernel,
+    side, cols = pl.pallas_call(
+        blocks_kernel,
         out_shape=(
-            pltpu.VMEM((devices, 4, 3 * blocks), jnp.float32),
-            pltpu.VMEM(positions.shape, jnp.float32),
-            pltpu.VMEM(velocities.shape, jnp.float32),
             pltpu.VMEM((8, blocks), jnp.float32),
             pltpu.VMEM((2, blocks, LANES), jnp.float32),
         ),
-        in_specs=[hbm] * 7 + [pl.BlockSpec(memory_space=pltpu.SMEM)],
-        out_specs=(vmem,) * 5,
+        in_specs=[hbm] * 4 + [smem],
+        out_specs=(vmem,) * 2,
         scratch_shapes=[
-            pltpu.VMEM((blocks, width), jnp.float32),
-            pltpu.VMEM((MOMENTS, blocks, LANES), jnp.float32),
             pltpu.VMEM((1, blocks), jnp.int32),
             pltpu.VMEM((halos // LANES, LANES), jnp.int32),
             pltpu.VMEM((3, blocks), jnp.int32),
             pltpu.VMEM((1, blocks), jnp.int32),
-            pltpu.SemaphoreType.DMA((3,)),
             pltpu.SemaphoreType.DMA((4,)),
         ],
-        compiler_params=pltpu.CompilerParams(vmem_limit_bytes=16 * 1024 * 1024),
-        name="moments",
+        compiler_params=pltpu.CompilerParams(vmem_limit_bytes=1024 * 1024),
+        cost_estimate=pl.CostEstimate(flops=FLOPS, bytes_accessed=BYTES, transcendentals=0),
+        name="blocks",
     )(
         *map(
             held,
             (
-                positions, velocities, masses, block_halo.reshape(1, blocks),
-                home_slot.reshape(halos // LANES, LANES), block_shift, block_live.reshape(1, blocks),
+                block_halo.reshape(1, blocks), home_slot.reshape(halos // LANES, LANES), block_shift,
+                block_live.reshape(1, blocks),
             ),
         ),
         block_count,
     )
+    send = pl.pallas_call(
+        moments_kernel,
+        out_shape=pltpu.VMEM((devices, 4, 3 * blocks), jnp.float32),
+        in_specs=[vmem] * 5,
+        out_specs=vmem,
+        scratch_shapes=[pltpu.VMEM((MOMENTS, blocks, LANES), jnp.float32)],
+        compiler_params=pltpu.CompilerParams(vmem_limit_bytes=8 * 1024 * 1024),
+        name="moments",
+    )(positions, velocities, masses, side, cols)
     recv = lax.all_to_all(send, AXES[::-1], 0, 0)
     table, kinetic, radial = pl.pallas_call(
         functools.partial(outputs_kernel, groups, domains, halos),
@@ -261,7 +261,7 @@
         ],
         compiler_params=pltpu.CompilerParams(vmem_limit_bytes=16 * 1024 * 1024),
         name="outputs",
-    )(recv, pos, vel, side, cols)
+    )(recv, positions, velocities, side, cols)
     return table, kinetic, radial
 
 

time: 20.4 us -> 20.4 us (level)
  Pallas kernels: 3.58 us -> 3.21 us
  local copies, waits for them, and re-layouts: 0 us -> 0.26 us
    pallas_call x1 -> x2, Pallas kernels: 2.02 us -> 1.65 us  [the longest x1 1.19 us: local(): pl.pallas_call(blocks_kernel, out_shape=(pltpu.VMEM((8, blocks), jnp.floa...]
    unnamed x0 -> x6, local copies, waits for them, and re-layouts: none -> 0.26 us
where the time goes in v4:
time: 20.4 us; the launch traced here: 20.2 us
  blocking collectives  15.4 us (75%)
  Pallas kernels  3.21 us (16%)
  between operations  1.32 us (6%)
  local copies, waits for them, and re-layouts  0.26 us (1%)
    all_to_all x1, blocking collectives, local(): recv = lax.all_to_all(send, AXES[::-1], 0, 0)  15.4 us
    pallas_call x1, Pallas kernels, local(): pl.pallas_call(functools.partial(outputs_kernel, groups, domains, halos),...  1.56 us
    pallas_call x1, Pallas kernels, local(): pl.pallas_call(blocks_kernel, out_shape=(pltpu.VMEM((8, blocks), jnp.floa...  1.19 us
    pallas_call x1, Pallas kernels, local(): pl.pallas_call(moments_kernel, out_shape=pltpu.VMEM((devices, 4, 3 * bloc...  0.47 us

profile of v4, /device:TPU:0, one launch (start us, length us, event | category | flops | bytes accessed | tf_op | source)
XLA Modules:
  0.0 20.2 jit_solution(17700914801406441932)
XLA Ops:
  1.3 0.0 copy-start
  1.3 0.0 copy-start.1
  1.3 0.0 copy-start.2
  1.3 1.2 %blocks.1 = (f32[8,128]{1,0:T(8,128)S(1)}, f32[2,128,128]{2,1,0:T(8,128)S(1)}) custom-call(s32[1,128]{1,0:T(1,128)} %bitcast.4, s32[32,128]{1,0:T(8,128)} %bitcast.3, s32[3,128]{1,0:T(4,128)} %shift_hbm.1, s32[1,128]{1,0:T(1,128)} %bitcast.5, s32[1]{0:T(128)S(6)} %copy.11.count_ref), custom_call_target="tpu_custom_call" | custom-call | flops 1000000000 | bytes 10000000 | tf_op jit(solution)/shard_map/blocks/pallas_call | solution.py:207
  2.5 0.0 copy-done
  2.5 0.2 %copy-done.1 = f32[3,128,512]{2,1,0:T(8,128)S(1)} copy-done((f32[3,128,512]{2,1,0:T(8,128)S(1)}, f32[3,128,512]{2,1,0:T(8,128)}, u32[]{:S(2)}) %copy-start.1) | copy-done | bytes 786456
  2.7 0.1 copy-done.2
  2.8 0.5 %moments.1 = f32[32,4,384]{2,1,0:T(4,128)S(1)} custom-call(f32[3,128,512]{2,1,0:T(8,128)S(1)} %copy-done, f32[3,128,512]{2,1,0:T(8,128)S(1)} %copy-done.1, f32[128,512]{1,0:T(8,128)S(1)} %copy-done.2, f32[8,128]{1,0:T(8,128)S(1)} %get-tuple-element.5.side_ref, f32[2,128,128]{2,1,0:T(8,128)S(1)} %get-tuple-element.6.cols_ref), custom_call_target="tpu_custom_call" | custom-call | tf_op jit(solution)/shard_map/moments/pallas_call | solution.py:235
  3.2 15.4 %all_to_all.5.recv_ref = f32[32,4,384]{2,1,0:T(4,128)S(1)} all-to-all(f32[32,4,384]{2,1,0:T(4,128)S(1)} %moments.1), channel_id=1, replica_groups=mesh['grp'=8,'dom'=4] {'dom','grp'}, dimensions={0} | all-to-all | bytes 393216 | tf_op jit(solution)/shard_map/all_to_all | solution.py:244
  18.6 1.6 %outputs.1 = (f32[11,128]{1,0:T(8,128)}, f32[128,512]{1,0:T(8,128)}, f32[128,512]{1,0:T(8,128)}) custom-call(f32[32,4,384]{2,1,0:T(4,128)S(1)} %all_to_all.5.recv_ref, f32[3,128,512]{2,1,0:T(8,128)S(1)} %copy-done, f32[3,128,512]{2,1,0:T(8,128)S(1)} %copy-done.1, f32[8,128]{1,0:T(8,128)S(1)} %get-tuple-element.5.side_ref, ...), custom_call_target="tpu_custom_call" | custom-call | tf_op jit(solution)/shard_map/outputs/pallas_call | solution.py:245
Async XLA Ops:
  1.3 1.2 %copy-start = (f32[3,128,512]{2,1,0:T(8,128)S(1)}, f32[3,128,512]{2,1,0:T(8,128)}, u32[]{:S(2)}) copy-start(f32[3,128,512]{2,1,0:T(8,128)} %pos_ref.3) | copy-start | bytes 2359300
  1.3 1.4 %copy-start.1 = (f32[3,128,512]{2,1,0:T(8,128)S(1)}, f32[3,128,512]{2,1,0:T(8,128)}, u32[]{:S(2)}) copy-start(f32[3,128,512]{2,1,0:T(8,128)} %vel_ref.3) | copy-start | bytes 2359300
  1.3 1.5 %copy-start.2 = (f32[128,512]{1,0:T(8,128)S(1)}, f32[128,512]{1,0:T(8,128)}, u32[]{:S(2)}) copy-start(f32[128,512]{1,0:T(8,128)} %mass_ref.1) | copy-start | bytes 786436

commit v5 on v3

--- a/solution.py
+++ b/solution.py
@@ -67,28 +67,42 @@
 
     lane = lax.broadcasted_iota(jnp.int32, (8, width), 1).astype(jnp.float32)
 
-    for copy in large:
+
+    def keep(k, rows, term):
+        part = term[:, 0:LANES]
+        for n in range(LANES, width, LANES):
+            part = part + term[:, n : n + LANES]
+        part_ref[k, rows] = part
+
+    def summed(k):
+        return jnp.sum(jnp.transpose(part_ref[k]), axis=0, keepdims=True)
+
+    raw = [None] * MOMENTS
+    for copy in large[:2]:
         copy.wait()
     for r in range(0, blocks, 8):
         rows = slice(r, r + 8)
-        edge = cols_ref[0, rows]
-        edge = jnp.concatenate([edge] * (width // LANES), axis=1)
+        edge = jnp.concatenate([cols_ref[0, rows]] * (width // LANES), axis=1)
         weight = jnp.where(lane < edge, mass_ref[rows], 0.0)
-        px, py, pz = (pos_ref[k, rows] for k in range(3))
         vx, vy, vz = (vel_ref[k, rows] for k in range(3))
         mx, my, mz = weight * vx, weight * vy, weight * vz
-        terms = (
-            weight, weight * px, weight * py, weight * pz, mx, my, mz,
-            mx * vx + my * vy + mz * vz,
-            py * mz - pz * my, pz * mx - px * mz, px * my - py * mx,
-        )
-        for k, term in enumerate(terms):
-            part = term[:, 0:LANES]
-            for n in range(LANES, width, LANES):
-                part = part + term[:, n : n + LANES]
-            part_ref[k, rows] = part
-
-    raw = [jnp.sum(jnp.transpose(part_ref[k]), axis=0, keepdims=True) for k in range(MOMENTS)]
+        mass_ref[rows] = weight
+        for k, term in ((0, weight), (4, mx), (5, my), (6, mz), (7, mx * vx + my * vy + mz * vz)):
+            keep(k, rows, term)
+    for k in (0, 4, 5, 6, 7):
+        raw[k] = summed(k)
+    large[2].wait()
+    for r in range(0, blocks, 8):
+        rows = slice(r, r + 8)
+        weight = mass_ref[rows]
+        vx, vy, vz = (vel_ref[k, rows] for k in range(3))
+        qx, qy, qz = (weight * pos_ref[k, rows] for k in range(3))
+        terms = (qx, qy, qz, qy * vz - qz * vy, qz * vx - qx * vz, qx * vy - qy * vx)
+        for k, term in zip((1, 2, 3, 8, 9, 10), terms):
+            keep(k, rows, term)
+    for k in (1, 2, 3, 8, 9, 10):
+        raw[k] = summed(k)
+
     w, rx, ry, rz, mx, my, mz, energy, ax, ay, az = raw
     table = rows_to_array(
         [
@@ -112,32 +126,40 @@
     group, domain = lax.axis_index("grp"), lax.axis_index("dom")
 
     near = []
-    for offset in sorted({o % groups for o in (-1, 0, 1)}):
+    offsets = list(dict.fromkeys((0, groups - 1, 1 % groups)))
+    for offset in offsets:
         source = lax.rem(group + offset, groups)
         for d in range(domains):
             part = recv_ref[d * groups + source]
             near.append(
                 jnp.concatenate([part[:, k * blocks : (k + 1) * blocks] for k in range(3)], axis=0)
             )
+    feeders = domains * len({0, groups - 1})
     base = ((group * domains + domain) * owned).astype(jnp.float32)
-    mine = cols_ref[1]
     own = lax.broadcasted_iota(jnp.int32, (owned, LANES), 0).astype(jnp.float32) + base
-    want = jnp.concatenate([mine, own], axis=0)
-    same = jnp.concatenate(
-        [jnp.where(want == rows[MOMENTS : MOMENTS + 1], 1.0, 0.0).astype(jnp.bfloat16) for rows in near],
-        axis=1,
-    )
     values = jnp.concatenate(near, axis=1)
     values = jnp.concatenate([values, jnp.zeros((4, values.shape[1]), jnp.float32)], axis=0)
     top = values.astype(jnp.bfloat16)
     rest = values - top.astype(jnp.float32)
     mid = rest.astype(jnp.bfloat16)
     last = (rest - mid.astype(jnp.float32)).astype(jnp.bfloat16)
-    sums = lax.dot_general(
-        jnp.concatenate([top, mid, last], axis=0), same, (((1,), (1,)), ((), ())),
-        preferred_element_type=jnp.float32,
-    )
-    sums = sums[0:16] + sums[16:32] + sums[32:48]
+    terms = jnp.concatenate([top, mid, last], axis=0)
+
+    def taken(want, sources):
+        same = jnp.concatenate(
+            [
+                jnp.where(want == rows[MOMENTS : MOMENTS + 1], 1.0, 0.0).astype(jnp.bfloat16)
+                for rows in near[:sources]
+            ],
+            axis=1,
+        )
+        out = lax.dot_general(
+            terms[:, 0 : sources * blocks], same, (((1,), (1,)), ((), ())),
+            preferred_element_type=jnp.float32,
+        )
+        return out[0:16] + out[16:32] + out[32:48]
+
+    sums = jnp.concatenate([taken(cols_ref[1], len(near)), taken(own, feeders)], axis=1)
 
     heavy = jnp.maximum(sums[0:1], 1.0)
     mean = sums[0:8] / heavy
@@ -154,6 +176,29 @@
         8, blocks,
     )
     stats_ref[...] = jnp.transpose(stats)
+
+    lane = lax.broadcasted_iota(jnp.int32, (8, width), 1).astype(jnp.float32)
+    step = blocks // OUT_CHUNKS
+
+    def leaving(c):
+        part = slice(c * step, (c + 1) * step)
+        return (
+            pltpu.make_async_copy(kin_ref.at[part], kin_hbm.at[part], sems.at[0, c]),
+            pltpu.make_async_copy(rad_ref.at[part], rad_hbm.at[part], sems.at[1, c]),
+        )
+
+    for c in range(OUT_CHUNKS):
+        for r in range(0, step, 8):
+            rows = slice(c * step + r, c * step + r + 8)
+            stat = stats_ref[rows]
+            alive = lane < jnp.concatenate([cols_ref[0, rows]] * (width // LANES), axis=1)
+            rx, ry, rz = (pos_ref[k, rows] - stat[:, k : k + 1] for k in range(3))
+            ox, oy, oz = (vel_ref[k, rows] - stat[:, k + 3 : k + 4] for k in range(3))
+            kinetic = (ox * ox + oy * oy + oz * oz) * stat[:, 6:7]
+            kin_ref[rows] = jnp.where(alive, kinetic, 0.0)
+            rad_ref[rows] = jnp.where(alive, rx * rx + ry * ry + rz * rz, 0.0)
+        for copy in leaving(c):
+            copy.start()
 
     whole = jnp.zeros((4, blocks), jnp.float32)
     for s in range(recv_ref.shape[0]):
@@ -168,30 +213,6 @@
     table_ref[8:11] = (sums[8:16, o] / heavy[:, o] - turn)[0:3]
     table_copy = pltpu.make_async_copy(table_ref, table_hbm, table_sem)
     table_copy.start()
-
-    lane = lax.broadcasted_iota(jnp.int32, (8, width), 1).astype(jnp.float32)
-    step = blocks // OUT_CHUNKS
-
-    def leaving(c):
-        part = pl.ds(pl.multiple_of(c * step, step), step)
-        return (
-            pltpu.make_async_copy(kin_ref.at[part], kin_hbm.at[part], sems.at[0, c]),
-            pltpu.make_async_copy(rad_ref.at[part], rad_hbm.at[part], sems.at[1, c]),
-        )
-
-    @pl.loop(0, OUT_CHUNKS)
-    def _(c):
-        for r in range(0, step, 8):
-            rows = pl.ds(pl.multiple_of(c * step + r, 8), 8)
-            stat = stats_ref[rows]
-            alive = lane < jnp.concatenate([cols_ref[0, rows]] * (width // LANES), axis=1)
-            rx, ry, rz = (pos_ref[k, rows] - stat[:, k : k + 1] for k in range(3))
-            ox, oy, oz = (vel_ref[k, rows] - stat[:, k + 3 : k + 4] for k in range(3))
-            kinetic = (ox * ox + oy * oy + oz * oz) * stat[:, 6:7]
-            kin_ref[rows] = jnp.where(alive, kinetic, 0.0)
-            rad_ref[rows] = jnp.where(alive, rx * rx + ry * ry + rz * rz, 0.0)
-        for copy in leaving(c):
-            copy.start()
 
     for c in range(OUT_CHUNKS):
         for copy in leaving(c):

time: 20.4 us -> 20.1 us (0.985)
  Pallas kernels: 3.58 us -> 3.29 us
where the time goes in v5:
time: 20.1 us; the launch traced here: 20 us
  blocking collectives  15.4 us (77%)
  Pallas kernels  3.29 us (16%)
  between operations  1.29 us (6%)
    all_to_all x1, blocking collectives, local(): recv = lax.all_to_all(send, AXES[::-1], 0, 0)  15.4 us
    pallas_call x1, Pallas kernels, local(): pl.pallas_call(moments_kernel, out_shape=(pltpu.VMEM((devices, 4, 3 * blo...  1.86 us
    pallas_call x1, Pallas kernels, local(): pl.pallas_call(functools.partial(outputs_kernel, groups, domains, halos),...  1.43 us

profile of v5, /device:TPU:0, one launch (start us, length us, event | category | flops | bytes accessed | tf_op | source)
XLA Modules:
  0.0 20.0 jit_solution(7319400466905499937)
XLA Ops:
  1.3 1.9 %moments.1 = (f32[32,4,384]{2,1,0:T(4,128)S(1)}, f32[3,128,512]{2,1,0:T(8,128)S(1)}, f32[3,128,512]{2,1,0:T(8,128)S(1)}, f32[8,128]{1,0:T(8,128)S(1)}, f32[2,128,128]{2,1,0:T(8,128)S(1)}) custom-call(f32[3,128,512]{2,1,0:T(8,128)} %pos_hbm.1, f32[3,128,512]{2,1,0:T(8,128)} %vel_hbm.1, f32[128,512]{1,0:T(8,128)} %mass_hbm.1, s32[1,128]{1,0:T(1,128)} %bitcast.4, ...), custom_call_target="tpu_custom_call" | custom-call | tf_op jit(solution)/shard_map/moments/pallas_call | solution.py:232
  3.1 15.4 %all_to_all.5.recv_ref = f32[32,4,384]{2,1,0:T(4,128)S(1)} all-to-all(f32[32,4,384]{2,1,0:T(4,128)S(1)} %get-tuple-element.8), channel_id=1, replica_groups=mesh['grp'=8,'dom'=4] {'dom','grp'}, dimensions={0} | all-to-all | bytes 393216 | tf_op jit(solution)/shard_map/all_to_all | solution.py:265
  18.5 1.4 %outputs.1 = (f32[11,128]{1,0:T(8,128)}, f32[128,512]{1,0:T(8,128)}, f32[128,512]{1,0:T(8,128)}) custom-call(f32[32,4,384]{2,1,0:T(4,128)S(1)} %all_to_all.5.recv_ref, f32[3,128,512]{2,1,0:T(8,128)S(1)} %get-tuple-element.9.pos_ref, f32[3,128,512]{2,1,0:T(8,128)S(1)} %get-tuple-element.10.vel_ref, f32[8,128]{1,0:T(8,128)S(1)} %get-tuple-element.11.side_ref, ...), custom_call_target="tpu_custom_call" | custom-call | tf_op jit(solution)/shard_map/outputs/pallas_call | solution.py:266

commit v6 on v5

--- a/solution.py
+++ b/solution.py
@@ -9,7 +9,7 @@
 
 EPSILON = 1e-06
 LANES = 128
-OUT_CHUNKS = 2
+OUT_CHUNKS = 4
 MOMENTS = 11
 AXES = ("grp", "dom")
 
@@ -159,19 +159,19 @@
         )
         return out[0:16] + out[16:32] + out[32:48]
 
-    sums = jnp.concatenate([taken(cols_ref[1], len(near)), taken(own, feeders)], axis=1)
-
-    heavy = jnp.maximum(sums[0:1], 1.0)
-    mean = sums[0:8] / heavy
-    cx, cy, cz, dx, dy, dz, energy = (mean[k : k + 1] for k in range(1, 8))
-    spread = energy - (dx * dx + dy * dy + dz * dz)
-
-    m = slice(0, blocks)
+    def means(sums):
+        heavy = jnp.maximum(sums[0:1], 1.0)
+        mean = sums[0:8] / heavy
+        cx, cy, cz, dx, dy, dz, energy = (mean[k : k + 1] for k in range(1, 8))
+        spread = energy - (dx * dx + dy * dy + dz * dz)
+        return heavy, mean, (cx, cy, cz), (dx, dy, dz), spread
+
+    _, _, centre, drift, spread = means(taken(cols_ref[1], len(near)))
     side = side_ref[...]
     stats = rows_to_array(
         [
-            cx[:, m] - side[1:2], cy[:, m] - side[2:3], cz[:, m] - side[3:4],
-            dx[:, m], dy[:, m], dz[:, m], 1.0 / (3.0 * spread[:, m] + EPSILON),
+            *(centre[k] - side[k + 1 : k + 2] for k in range(3)),
+            *drift, 1.0 / (3.0 * spread + EPSILON),
         ],
         8, blocks,
     )
@@ -197,20 +197,20 @@
             kinetic = (ox * ox + oy * oy + oz * oz) * stat[:, 6:7]
             kin_ref[rows] = jnp.where(alive, kinetic, 0.0)
             rad_ref[rows] = jnp.where(alive, rx * rx + ry * ry + rz * rz, 0.0)
-        for copy in leaving(c):
-            copy.start()
+        for k, copy in enumerate(leaving(c)):
+            copy.start(priority=k)
 
     whole = jnp.zeros((4, blocks), jnp.float32)
     for s in range(recv_ref.shape[0]):
         whole = whole + recv_ref[s, :, 0:blocks]
     total = jnp.sum(whole[0:1], axis=1, keepdims=True)
-    o = slice(blocks, blocks + owned)
-    share = sums[0:1, o] * float(halos) / total
+    sums = taken(own, feeders)
+    heavy, mean, (cx, cy, cz), (dx, dy, dz), spread = means(sums)
+    share = sums[0:1] * float(halos) / total
     at = lax.broadcasted_iota(jnp.int32, (8, owned), 0)
-    table_ref[0:8] = jnp.where(at == 0, share, jnp.where(at == 7, spread[:, o], mean[:, o]))
-    cx, cy, cz, dx, dy, dz = (v[:, o] for v in (cx, cy, cz, dx, dy, dz))
+    table_ref[0:8] = jnp.where(at == 0, share, jnp.where(at == 7, spread, mean))
     turn = rows_to_array([cy * dz - cz * dy, cz * dx - cx * dz, cx * dy - cy * dx], 8, owned)
-    table_ref[8:11] = (sums[8:16, o] / heavy[:, o] - turn)[0:3]
+    table_ref[8:11] = (sums[8:16] / heavy - turn)[0:3]
     table_copy = pltpu.make_async_copy(table_ref, table_hbm, table_sem)
     table_copy.start()
 

time: 20.1 us -> 20.1 us (level)
  no operation moved by 1% of the time
where the time goes in v6:
time: 20.1 us; the launch traced here: 20 us
  blocking collectives  15.4 us (77%)
  Pallas kernels  3.28 us (16%)
  between operations  1.29 us (6%)
    all_to_all x1, blocking collectives, local(): recv = lax.all_to_all(send, AXES[::-1], 0, 0)  15.4 us
    pallas_call x1, Pallas kernels, local(): pl.pallas_call(moments_kernel, out_shape=(pltpu.VMEM((devices, 4, 3 * blo...  1.86 us
    pallas_call x1, Pallas kernels, local(): pl.pallas_call(functools.partial(outputs_kernel, groups, domains, halos),...  1.42 us

profile of v6, /device:TPU:0, one launch (start us, length us, event | category | flops | bytes accessed | tf_op | source)
XLA Modules:
  0.0 20.0 jit_solution(1758976171018633083)
XLA Ops:
  1.3 1.9 %moments.1 = (f32[32,4,384]{2,1,0:T(4,128)S(1)}, f32[3,128,512]{2,1,0:T(8,128)S(1)}, f32[3,128,512]{2,1,0:T(8,128)S(1)}, f32[8,128]{1,0:T(8,128)S(1)}, f32[2,128,128]{2,1,0:T(8,128)S(1)}) custom-call(f32[3,128,512]{2,1,0:T(8,128)} %pos_hbm.1, f32[3,128,512]{2,1,0:T(8,128)} %vel_hbm.1, f32[128,512]{1,0:T(8,128)} %mass_hbm.1, s32[1,128]{1,0:T(1,128)} %bitcast.4, ...), custom_call_target="tpu_custom_call" | custom-call | tf_op jit(solution)/shard_map/moments/pallas_call | solution.py:232
  3.1 15.4 %all_to_all.5.recv_ref = f32[32,4,384]{2,1,0:T(4,128)S(1)} all-to-all(f32[32,4,384]{2,1,0:T(4,128)S(1)} %get-tuple-element.8), channel_id=1, replica_groups=mesh['grp'=8,'dom'=4] {'dom','grp'}, dimensions={0} | all-to-all | bytes 393216 | tf_op jit(solution)/shard_map/all_to_all | solution.py:265
  18.5 1.4 %outputs.1 = (f32[11,128]{1,0:T(8,128)}, f32[128,512]{1,0:T(8,128)}, f32[128,512]{1,0:T(8,128)}) custom-call(f32[32,4,384]{2,1,0:T(4,128)S(1)} %all_to_all.5.recv_ref, f32[3,128,512]{2,1,0:T(8,128)S(1)} %get-tuple-element.9.pos_ref, f32[3,128,512]{2,1,0:T(8,128)S(1)} %get-tuple-element.10.vel_ref, f32[8,128]{1,0:T(8,128)S(1)} %get-tuple-element.11.side_ref, ...), custom_call_target="tpu_custom_call" | custom-call | tf_op jit(solution)/shard_map/outputs/pallas_call | solution.py:266

commit v7 on v6

--- a/solution.py
+++ b/solution.py
@@ -9,7 +9,7 @@
 
 EPSILON = 1e-06
 LANES = 128
-OUT_CHUNKS = 4
+OUT_CHUNKS = 2
 MOMENTS = 11
 AXES = ("grp", "dom")
 
@@ -42,8 +42,9 @@
             ((mass_hbm, mass_ref), (vel_hbm, vel_ref), (pos_hbm, pos_ref))
         )
     ]
-    for copy in small + large:
+    for copy in small + large[:2]:
         copy.start()
+    large[2].start(priority=1)
 
     for copy in small:
         copy.wait()

time: 20.1 us -> 20.1 us (level)
  no operation moved by 1% of the time
where the time goes in v7:
time: 20.1 us; the launch traced here: 20 us
  blocking collectives  15.4 us (77%)
  Pallas kernels  3.29 us (16%)
  between operations  1.29 us (6%)
    all_to_all x1, blocking collectives, local(): recv = lax.all_to_all(send, AXES[::-1], 0, 0)  15.4 us
    pallas_call x1, Pallas kernels, local(): pl.pallas_call(moments_kernel, out_shape=(pltpu.VMEM((devices, 4, 3 * blo...  1.86 us
    pallas_call x1, Pallas kernels, local(): pl.pallas_call(functools.partial(outputs_kernel, groups, domains, halos),...  1.43 us

profile of v7, /device:TPU:0, one launch (start us, length us, event | category | flops | bytes accessed | tf_op | source)
XLA Modules:
  0.0 20.0 jit_solution(17120142384172065451)
XLA Ops:
  1.3 1.9 %moments.1 = (f32[32,4,384]{2,1,0:T(4,128)S(1)}, f32[3,128,512]{2,1,0:T(8,128)S(1)}, f32[3,128,512]{2,1,0:T(8,128)S(1)}, f32[8,128]{1,0:T(8,128)S(1)}, f32[2,128,128]{2,1,0:T(8,128)S(1)}) custom-call(f32[3,128,512]{2,1,0:T(8,128)} %pos_hbm.1, f32[3,128,512]{2,1,0:T(8,128)} %vel_hbm.1, f32[128,512]{1,0:T(8,128)} %mass_hbm.1, s32[1,128]{1,0:T(1,128)} %bitcast.4, ...), custom_call_target="tpu_custom_call" | custom-call | tf_op jit(solution)/shard_map/moments/pallas_call | solution.py:233
  3.1 15.4 %all_to_all.5.recv_ref = f32[32,4,384]{2,1,0:T(4,128)S(1)} all-to-all(f32[32,4,384]{2,1,0:T(4,128)S(1)} %get-tuple-element.8), channel_id=1, replica_groups=mesh['grp'=8,'dom'=4] {'dom','grp'}, dimensions={0} | all-to-all | bytes 393216 | tf_op jit(solution)/shard_map/all_to_all | solution.py:266
  18.5 1.4 %outputs.1 = (f32[11,128]{1,0:T(8,128)}, f32[128,512]{1,0:T(8,128)}, f32[128,512]{1,0:T(8,128)}) custom-call(f32[32,4,384]{2,1,0:T(4,128)S(1)} %all_to_all.5.recv_ref, f32[3,128,512]{2,1,0:T(8,128)S(1)} %get-tuple-element.9.pos_ref, f32[3,128,512]{2,1,0:T(8,128)S(1)} %get-tuple-element.10.vel_ref, f32[8,128]{1,0:T(8,128)S(1)} %get-tuple-element.11.side_ref, ...), custom_call_target="tpu_custom_call" | custom-call | tf_op jit(solution)/shard_map/outputs/pallas_call | solution.py:267
